TPU v7x, 32 devices: a whole 2x2x4 slice. The times are simulated.
32 devices in a mesh: dp: 4 (over y, x), vocab: 8 (over z, core).
Axes of the slice: x: 2, y: 2, z: 4, core: 2. Of those that a mesh axis runs over, the one named last changes fastest.
Arguments:
- logits: bfloat16 [32, 8, 152064], P('dp', None, 'vocab'), may hold values from -40 to 250
- draft_probs: bfloat16 [32, 8, 152064], P('dp', None, 'vocab'), may hold values from 5.9185606e-07 to 1, as said below
- draft_tokens: int32 [32, 8], P('dp'), may hold values from 0 to 152063
- draft_lengths: int32 [32], P('dp'), may hold values from 1 to 8
- owner_group: int32 [32], P('dp'), may hold values from 0 to 3, as said below
Outputs:
- correction: bfloat16 [64, 152064], P('dp', 'vocab')
- accept_ratio: float32 [64, 8], P('dp')
- expected_accepted: float32 [64], P('dp')
Inputs may be any that keep to these rules, and one draw needn't show every extreme that they name: Each row of draft_probs is a distribution over the whole vocabulary whose entries are all positive. `owner_group`: no group hands more than 4 sequences to one group; some group receives exactly 4 sequences from every group.
All inputs are finite; a program needn't handle non-finite values.
Results may differ from a plain program's by a relative error of at most 0.001.
Values may be sent and summed in bfloat16 or wider, within the bound.
A program may use at most 64 MiB of HBM per device.

v0:
```python
import jax
import jax.numpy as jnp
from jax import lax
from jax.sharding import PartitionSpec as P

mixing = 0.1


def verify(logits, draft_probs, tokens, lengths):
    scores = logits.astype(jnp.float32)
    shard_width = scores.shape[2]
    column = (
        lax.broadcasted_iota(jnp.int32, scores.shape, 2) + lax.axis_index("vocab") * shard_width
    )
    is_drafted = column == tokens[:, :, None]
    proposal = draft_probs.astype(jnp.float32)
    drafted_local = jnp.sum(jnp.where(is_drafted, proposal, 0.0), axis=2)
    top = lax.pmax(jnp.max(scores, axis=2), "vocab")
    shifted = jnp.exp(scores - top[:, :, None])
    row_total, chosen, drafted = lax.psum(
        (
            jnp.sum(shifted, axis=2),
            jnp.sum(jnp.where(is_drafted, shifted, 0.0), axis=2),
            drafted_local,
        ),
        "vocab",
    )
    target = shifted / row_total[:, :, None]
    excess = jnp.maximum(target - proposal, 0.0)
    spread = lax.psum(jnp.sum(excess, axis=2), "vocab")
    residual = (excess + mixing * target) / (spread + mixing)[:, :, None]
    position = lax.broadcasted_iota(jnp.int32, tokens.shape, 1)
    is_live = position < lengths[:, None]
    safe_draft = jnp.where(is_live, drafted, 1.0)
    accept = jnp.where(is_live, jnp.minimum(1.0, chosen / row_total / safe_draft), 0.0)
    survive = jnp.cumprod(accept, axis=1)
    before = jnp.concatenate([jnp.ones_like(survive[:, :1]), survive[:, :-1]], axis=1)
    weight = jnp.where(is_live, before * (1.0 - accept), 0.0)
    corrected = jnp.sum(weight[:, :, None] * residual, axis=1).astype(jnp.bfloat16)
    expected = jnp.sum(survive, axis=1)
    return (corrected, accept, expected)


def routing(owners, capacity, groups):
    seq_count = owners.shape[0]
    earlier = lax.broadcasted_iota(jnp.int32, (seq_count, seq_count), 1) < lax.broadcasted_iota(
        jnp.int32, (seq_count, seq_count), 0
    )
    same = owners[:, None] == owners[None, :]
    slot_rank = jnp.sum(jnp.where(same & earlier, 1, 0), axis=1)
    target_slot = owners * capacity + slot_rank
    slot_rows = lax.broadcasted_iota(jnp.int32, (groups * capacity, seq_count), 0)
    return slot_rows == target_slot[None, :]


def body(logits, draft_probs, draft_tokens, draft_lengths, owner_group):
    groups = lax.axis_size("dp")
    seq_count = owner_group.shape[0]
    capacity = max(2, 2 * seq_count // groups)
    select = routing(owner_group, capacity, groups)
    picker = select.astype(jnp.bfloat16)
    corrected, accept, expected = verify(logits, draft_probs, draft_tokens, draft_lengths)
    outgoing = jnp.dot(picker, corrected, preferred_element_type=jnp.float32).astype(jnp.bfloat16)
    correction = lax.all_to_all(outgoing, "dp", split_axis=0, concat_axis=0, tiled=True)
    sent_accept = jnp.sum(jnp.where(select[:, :, None], accept[None, :, :], 0.0), axis=1)
    sent_expected = jnp.sum(jnp.where(select, expected[None, :], 0.0), axis=1)
    accept_ratio, expected_accepted = (
        lax.all_to_all(sent_accept, "dp", split_axis=0, concat_axis=0, tiled=True),
        lax.all_to_all(sent_expected, "dp", split_axis=0, concat_axis=0, tiled=True),
    )
    return (correction, accept_ratio, expected_accepted)


def solution(mesh):
    placed = (P("dp", None, "vocab"), P("dp", None, "vocab"), P("dp", None), P("dp"), P("dp"))
    return jax.shard_map(
        body,
        mesh=mesh,
        in_specs=placed,
        out_specs=(P("dp", "vocab"), P("dp", None), P("dp")),
        check_vma=False,
    )
```

profile of v0, /device:TPU:0, one launch (start us, length us, event | category | flops | bytes accessed | tf_op | source)
XLA Modules:
  0.0 98.8 jit_solution(12494934219520476122)
XLA Ops:
  0.7 1.0 %select_reduce_fusion.2 = s32[8]{0:T(128)S(1)} fusion(s32[8]{0:T(128)} %param.9), kind=kLoop, calls=%fused_computation.19 | loop fusion | flops 312 | bytes 64 | tf_op jit(solution)/shard_map/reduce_sum | solution.py:50
  1.7 0.7 multiply_add_fusion
  2.3 2.2 %reduce_max.14 = bf16[8,8]{1,0:T(8,128)(2,1)S(1)} reduce(bf16[8,8,19008]{2,1,0:T(8,128)(2,1)} %param.5, bf16[]{:T(256)} %constant.14.clone.1), dimensions={2}, to_apply=%region_1.2 | reduce | flops 1216448 | bytes 2433154 | tf_op jit(solution)/shard_map/reduce_max | solution.py:18
  4.5 18.1 %pmax.7 = f32[8,8]{1,0:T(8,128)S(1)} all-reduce(bf16[8,8]{1,0:T(8,128)(2,1)S(1)} %reduce_max.14), channel_id=1, replica_groups=mesh['dp'=4,'vocab'=8] {'vocab'}, use_global_device_ids=true, to_apply=%region_2.3 | all-reduce | flops 64 | bytes 384 | tf_op jit(solution)/shard_map/pmax | solution.py:18
  22.6 1.7 %fusion.1 = (f32[8,8]{1,0:T(8,128)S(1)}, f32[8,8]{1,0:T(8,128)S(1)}) fusion(bf16[8,8,19008]{2,1,0:T(8,128)(2,1)S(1)} %copy-done, f32[8,8]{1,0:T(8,128)S(1)} %pmax.7, s32[8,8]{1,0:T(8,128)S(1)} %copy-done.1, s32[19008]{0:T(1024)S(1)} %iota_add_fusion), kind=kLoop, calls=%fused_computation.5 | loop fusion | flops 7298944 | bytes 2510080 | tf_op jit(solution)/shard_map/reduce_sum | solution.py:23
  24.3 13.6 %psum.29 = f32[8,8]{1,0:T(8,128)S(1)} all-reduce(f32[8,8]{1,0:T(8,128)S(1)} %get-tuple-element.13), channel_id=1, replica_groups=mesh['dp'=4,'vocab'=8] {'vocab'}, use_global_device_ids=true, to_apply=%region_6.7 | all-reduce | flops 64 | bytes 512 | tf_op jit(solution)/shard_map/psum | solution.py:20
  37.9 3.9 %fusion.2 = (f32[8,8]{1,0:T(8,128)S(1)}, f32[8,8]{1,0:T(8,128)S(1)}) fusion(bf16[8,8,19008]{2,1,0:T(8,128)(2,1)} %param.6, s32[8,8]{1,0:T(8,128)S(1)} %copy-done.1, s32[19008]{0:T(1024)S(1)} %iota_add_fusion, f32[8,8]{1,0:T(8,128)S(1)} %psum.29, f32[8,8]{1,0:T(8,128)S(1)} %pmax.7, bf16[8,8,19008]{2,1,0:T(8,128)(2,1)S(1)} %copy-done), kind=kLoop, calls=%fused_computation.6 | loop fusion | flops 12164992 | bytes 4943360 | tf_op jit(solution)/shard_map/reduce_sum | solution.py:17
  41.8 25.9 %all-reduce.1 = (f32[8,8]{1,0:T(8,128)S(1)}, f32[8,8]{1,0:T(8,128)S(1)}, f32[8,8]{1,0:T(8,128)S(1)}) all-reduce(f32[8,8]{1,0:T(8,128)S(1)} %get-tuple-element.15, f32[8,8]{1,0:T(8,128)S(1)} %get-tuple-element.12, f32[8,8]{1,0:T(8,128)S(1)} %get-tuple-element.14), channel_id=1, replica_groups=mesh['dp'=4,'vocab'=8] {'vocab'}, use_global_device_ids=true, to_apply=%region_11.12 | all-reduce | flops 192 | bytes 1536 | tf_op jit(solution)/shard_map/psum | solution.py:30
  67.8 0.2 reduce_window.9
  68.2 0.7 all_to_all.30
  68.8 3.7 %all-to-all-start.2 = ((f32[4,4,1]{1,2,0:T(1,128)}), f32[4,4,1]{1,2,0:T(1,128)S(1)}, u32[]{:S(2)}, u32[]{:S(2)}) async-start(f32[4,4,1]{1,2,0:T(1,128)} %bitcast.2), calls=%async_computation.2 | async-start | bytes 4096 | tf_op jit(solution)/shard_map/all_to_all | solution.py:69
  72.8 0.7 copy.11
  73.5 4.8 %multiply_reduce_fusion = bf16[8,19008]{1,0:T(8,128)(2,1)S(1)} fusion(bf16[8,8,19008]{2,1,0:T(8,128)(2,1)} %param.6, bf16[8,8,19008]{2,1,0:T(8,128)(2,1)S(1)} %copy-done, f32[8,8]{1,0:T(8,128)S(1)} %get-tuple-element.20, f32[8,8]{1,0:T(8,128)S(1)} %psum.29, f32[8,8]{1,0:T(8,128)S(1)} %multiply_select_fusion, f32[8,8]{1,0:T(8,128)S(1)} %pmax.7), kind=kLoop, calls=%fused_computation.7 | loop fusion | flops 13229568 | bytes 5171200 | tf_op jit(solution)/shard_map/reduce_sum | solution.py:39
  78.3 4.2 %all-to-all-start.1 = ((f32[4,4,8]{2,1,0:T(4,128)}), f32[4,4,8]{2,1,0:T(4,128)S(1)}, u32[]{:S(2)}, u32[]{:S(2)}) async-start(f32[4,4,8]{2,1,0:T(4,128)} %bitcast), calls=%async_computation.1 | async-start | bytes 16384 | tf_op jit(solution)/shard_map/all_to_all | solution.py:68
  82.5 0.4 convolution_convert_fusion
  82.9 1.0 all_to_all.24
  83.9 3.3 %all-to-all-done.1 = f32[4,4,8]{2,1,0:T(4,128)S(1)} async-done(((f32[4,4,8]{2,1,0:T(4,128)}), f32[4,4,8]{2,1,0:T(4,128)S(1)}, u32[]{:S(2)}, u32[]{:S(2)}) %all-to-all-start.1) | async-done | bytes 544 | tf_op jit(solution)/shard_map/all_to_all | solution.py:68
  87.2 3.5 %all-to-all-start = ((bf16[4,4,19008]{2,1,0:T(4,128)(2,1)}), bf16[4,4,19008]{2,1,0:T(4,128)(2,1)S(1)}, u32[]{:S(2)}, u32[]{:S(2)}) async-start(bf16[4,4,19008]{2,1,0:T(4,128)(2,1)} %all_to_all.24), calls=%async_computation | async-start | bytes 1220608 | tf_op jit(solution)/shard_map/all_to_all | solution.py:64
  90.6 0.5 broadcast.32
  91.2 0.7 reduce.4
  91.8 0.6 all_to_all.32
  92.4 0.7 copy.13
  93.1 4.6 %all-to-all-done = bf16[4,4,19008]{2,1,0:T(4,128)(2,1)S(1)} async-done(((bf16[4,4,19008]{2,1,0:T(4,128)(2,1)}), bf16[4,4,19008]{2,1,0:T(4,128)(2,1)S(1)}, u32[]{:S(2)}, u32[]{:S(2)}) %all-to-all-start) | async-done | bytes 608288 | tf_op jit(solution)/shard_map/all_to_all | solution.py:64
  97.7 1.1 %all_to_all.26 = bf16[16,19008]{1,0:T(8,128)(2,1)} reshape(bf16[4,4,19008]{2,1,0:T(4,128)(2,1)S(1)} %all-to-all-done) | data formatting | bytes 1216512 | tf_op jit(solution)/shard_map/all_to_all | solution.py:64
  (14 shorter events, 0.5 us)
Async XLA Ops:
  0.6 22.0 %copy-start = (bf16[8,8,19008]{2,1,0:T(8,128)(2,1)S(1)}, bf16[8,8,19008]{2,1,0:T(8,128)(2,1)}, u32[]{:S(2)}) copy-start(bf16[8,8,19008]{2,1,0:T(8,128)(2,1)} %param.5) | copy-start | bytes 7299076
  0.6 22.0 %copy-start.1 = (s32[8,8]{1,0:T(8,128)S(1)}, s32[8,8]{1,0:T(8,128)}, u32[]{:S(2)}) copy-start(s32[8,8]{1,0:T(8,128)} %param.7) | copy-start | bytes 772
  37.9 29.8 %copy-start.2 = (s32[8]{0:T(128)S(1)}, s32[8]{0:T(128)}, u32[]{:S(2)}) copy-start(s32[8]{0:T(128)} %param.8) | copy-start | bytes 100
  68.8 9.4 %all-to-all-start.2 = ((f32[4,4,1]{1,2,0:T(1,128)}), f32[4,4,1]{1,2,0:T(1,128)S(1)}, u32[]{:S(2)}, u32[]{:S(2)}) async-start(f32[4,4,1]{1,2,0:T(1,128)} %bitcast.2), calls=%async_computation.2 | async-start | bytes 4096 | tf_op jit(solution)/shard_map/all_to_all | solution.py:69
  78.3 8.9 %all-to-all-start.1 = ((f32[4,4,8]{2,1,0:T(4,128)}), f32[4,4,8]{2,1,0:T(4,128)S(1)}, u32[]{:S(2)}, u32[]{:S(2)}) async-start(f32[4,4,8]{2,1,0:T(4,128)} %bitcast), calls=%async_computation.1 | async-start | bytes 16384 | tf_op jit(solution)/shard_map/all_to_all | solution.py:68
  87.2 10.5 %all-to-all-start = ((bf16[4,4,19008]{2,1,0:T(4,128)(2,1)}), bf16[4,4,19008]{2,1,0:T(4,128)(2,1)S(1)}, u32[]{:S(2)}, u32[]{:S(2)}) async-start(bf16[4,4,19008]{2,1,0:T(4,128)(2,1)} %all_to_all.24), calls=%async_computation | async-start | bytes 1220608 | tf_op jit(solution)/shard_map/all_to_all | solution.py:64
where the time goes:
time: 99.2 us; the launch traced here: 98.8 us
  blocking collectives  57.6 us (58%)
  other arithmetic  15.6 us (16%)
  starting transfers between devices  11.4 us (11%)
  waiting for transfers between devices  7.9 us (8%)
  local copies, waits for them, and re-layouts  5.16 us (5%)
    psum x1, blocking collectives, verify(): spread = lax.psum(jnp.sum(excess, axis=2), 'vocab')  25.9 us
    pmax x1, blocking collectives, verify(): top = lax.pmax(jnp.max(scores, axis=2), 'vocab')  18.1 us
    psum x1, blocking collectives, verify(): lax.psum((jnp.sum(shifted, axis=2), jnp.sum(jnp.where(is_drafted, shifted...  13.6 us
    reduce_sum x1, other arithmetic, verify(): jnp.sum(weight[:, :, None] * residual, axis=1).astype(jnp.bfloat16)  4.79 us
    all_to_all x1, waiting for transfers between devices, body(): lax.all_to_all(outgoing, 'dp', split_axis=0, concat_axis=0, tiled=True)  4.61 us
    all_to_all x1, starting transfers between devices, body(): lax.all_to_all(sent_accept, 'dp', split_axis=0, concat_axis=0, tiled=True)  4.2 us
    reduce_sum x1, other arithmetic, verify(): drafted_local = jnp.sum(jnp.where(is_drafted, proposal, 0.0), axis=2)  3.89 us
    all_to_all x1, starting transfers between devices, body(): lax.all_to_all(sent_expected, 'dp', split_axis=0, concat_axis=0, tiled=True)  3.72 us
  transfers between devices with their start and end apart: 3, of which 2 were waited for; matrix products, arithmetic and copies ran while one was open for 8% of the time, Pallas kernels for 0%

commit v1 on v0

--- a/solution.py
+++ b/solution.py
@@ -27,7 +27,9 @@
     )
     target = shifted / row_total[:, :, None]
     excess = jnp.maximum(target - proposal, 0.0)
-    spread = lax.psum(jnp.sum(excess, axis=2), "vocab")
+    block = jnp.sum(excess, axis=2)
+    shards = lax.all_gather(block, "vocab")
+    spread = jnp.sum(shards, axis=0)
     residual = (excess + mixing * target) / (spread + mixing)[:, :, None]
     position = lax.broadcasted_iota(jnp.int32, tokens.shape, 1)
     is_live = position < lengths[:, None]

time: 99.2 us -> 103 us (1.038)
  blocking collectives: 57.6 us -> 59.6 us
  waiting for transfers between devices: 7.9 us -> 9.12 us
    psum x1 -> x0, blocking collectives: 25.9 us -> none  [verify(): spread = lax.psum(jnp.sum(excess, axis=2), 'vocab')]
    all_gather x0 -> x1, blocking collectives: none -> 14.1 us  [verify(): shards = lax.all_gather(block, 'vocab')]
    psum x1 -> x2, blocking collectives: 13.6 us -> 27.5 us  [verify(): lax.psum((jnp.sum(shifted, axis=2), jnp.sum(jnp.where(is_drafted, shifted...]
    all_to_all x1, waiting for transfers between devices: 4.61 us -> 5.83 us  [body(): lax.all_to_all(outgoing, 'dp', split_axis=0, concat_axis=0, tiled=True)]
where the time goes in v1:
time: 103 us; the launch traced here: 102 us
  blocking collectives  59.6 us (58%)
  other arithmetic  15.6 us (15%)
  starting transfers between devices  11.4 us (11%)
  waiting for transfers between devices  9.12 us (9%)
  local copies, waits for them, and re-layouts  5.16 us (5%)
    psum x2, blocking collectives, verify(): lax.psum((jnp.sum(shifted, axis=2), jnp.sum(jnp.where(is_drafted, shifted...  27.5 us
    pmax x1, blocking collectives, verify(): top = lax.pmax(jnp.max(scores, axis=2), 'vocab')  18.1 us
    all_gather x1, blocking collectives, verify(): shards = lax.all_gather(block, 'vocab')  14.1 us
    all_to_all x1, waiting for transfers between devices, body(): lax.all_to_all(outgoing, 'dp', split_axis=0, concat_axis=0, tiled=True)  5.83 us
    reduce_sum x1, other arithmetic, verify(): jnp.sum(weight[:, :, None] * residual, axis=1).astype(jnp.bfloat16)  4.8 us
    all_to_all x1, starting transfers between devices, body(): lax.all_to_all(sent_accept, 'dp', split_axis=0, concat_axis=0, tiled=True)  4.2 us
    reduce_sum x1, other arithmetic, verify(): drafted_local = jnp.sum(jnp.where(is_drafted, proposal, 0.0), axis=2)  3.89 us
    all_to_all x1, starting transfers between devices, body(): lax.all_to_all(sent_expected, 'dp', split_axis=0, concat_axis=0, tiled=True)  3.72 us
  transfers between devices with their start and end apart: 3, of which 2 were waited for; matrix products, arithmetic and copies ran while one was open for 8% of the time, Pallas kernels for 0%

profile of v1, /device:TPU:0, one launch (start us, length us, event | category | flops | bytes accessed | tf_op | source)
XLA Modules:
  0.0 102.1 jit_solution(3289026962107947196)
XLA Ops:
  0.7 1.0 select_reduce_fusion.2
  1.7 0.7 multiply_add_fusion
  2.3 2.2 %reduce_max.14 = bf16[8,8]{1,0:T(8,128)(2,1)S(1)} reduce(bf16[8,8,19008]{2,1,0:T(8,128)(2,1)} %param.5, bf16[]{:T(256)} %constant.14.clone.1), dimensions={2}, to_apply=%region_1.2 | reduce | flops 1216448 | bytes 2433154 | tf_op jit(solution)/shard_map/reduce_max | solution.py:18
  4.5 18.1 %pmax.7 = f32[8,8]{1,0:T(8,128)S(1)} all-reduce(bf16[8,8]{1,0:T(8,128)(2,1)S(1)} %reduce_max.14), channel_id=1, replica_groups=mesh['dp'=4,'vocab'=8] {'vocab'}, use_global_device_ids=true, to_apply=%region_2.3 | all-reduce | flops 64 | bytes 384 | tf_op jit(solution)/shard_map/pmax | solution.py:18
  22.6 1.7 %fusion.1 = (f32[8,8]{1,0:T(8,128)S(1)}, f32[8,8]{1,0:T(8,128)S(1)}) fusion(bf16[8,8,19008]{2,1,0:T(8,128)(2,1)S(1)} %copy-done, f32[8,8]{1,0:T(8,128)S(1)} %pmax.7, s32[8,8]{1,0:T(8,128)S(1)} %copy-done.1, s32[19008]{0:T(1024)S(1)} %iota_add_fusion), kind=kLoop, calls=%fused_computation.5 | loop fusion | flops 7298944 | bytes 2510080 | tf_op jit(solution)/shard_map/reduce_sum | solution.py:23
  24.3 13.6 %psum.22 = f32[8,8]{1,0:T(8,128)S(1)} all-reduce(f32[8,8]{1,0:T(8,128)S(1)} %get-tuple-element.13), channel_id=1, replica_groups=mesh['dp'=4,'vocab'=8] {'vocab'}, use_global_device_ids=true, to_apply=%region_6.7 | all-reduce | flops 64 | bytes 512 | tf_op jit(solution)/shard_map/psum | solution.py:20
  37.9 3.9 %fusion.2 = (f32[8,8]{1,0:T(8,128)S(1)}, f32[8,8]{1,0:T(8,128)S(1)}) fusion(bf16[8,8,19008]{2,1,0:T(8,128)(2,1)} %param.6, s32[8,8]{1,0:T(8,128)S(1)} %copy-done.1, s32[19008]{0:T(1024)S(1)} %iota_add_fusion, f32[8,8]{1,0:T(8,128)S(1)} %psum.22, f32[8,8]{1,0:T(8,128)S(1)} %pmax.7, bf16[8,8,19008]{2,1,0:T(8,128)(2,1)S(1)} %copy-done), kind=kLoop, calls=%fused_computation.6 | loop fusion | flops 12164992 | bytes 4943360 | tf_op jit(solution)/shard_map/reduce_sum | solution.py:17
  41.8 13.9 %all-reduce.1 = (f32[8,8]{1,0:T(8,128)S(1)}, f32[8,8]{1,0:T(8,128)S(1)}) all-reduce(f32[8,8]{1,0:T(8,128)S(1)} %get-tuple-element.12, f32[8,8]{1,0:T(8,128)S(1)} %get-tuple-element.14), channel_id=1, replica_groups=mesh['dp'=4,'vocab'=8] {'vocab'}, use_global_device_ids=true, to_apply=%region_4.5 | all-reduce | flops 128 | bytes 1024 | tf_op jit(solution)/shard_map/psum | solution.py:20
  56.2 0.7 all_to_all.30
  56.8 3.7 %all-to-all-start.2 = ((f32[4,4,1]{1,2,0:T(1,128)}), f32[4,4,1]{1,2,0:T(1,128)S(1)}, u32[]{:S(2)}, u32[]{:S(2)}) async-start(f32[4,4,1]{1,2,0:T(1,128)} %bitcast.3), calls=%async_computation.2 | async-start | bytes 4096 | tf_op jit(solution)/shard_map/all_to_all | solution.py:71
  60.8 0.7 copy.11
  61.5 14.1 %all-gather = f32[64,8]{1,0:T(8,128)S(1)} all-gather(f32[8,8]{1,0:T(8,128)S(1)} %get-tuple-element.15), channel_id=2, replica_groups=mesh['dp'=4,'vocab'=8] {'vocab'}, dimensions={0}, use_global_device_ids=true | all-gather | bytes 2304 | tf_op jit(solution)/shard_map/all_gather | solution.py:31
  75.6 4.8 %multiply_reduce_fusion = bf16[8,19008]{1,0:T(8,128)(2,1)S(1)} fusion(bf16[8,8,19008]{2,1,0:T(8,128)(2,1)} %param.6, bf16[8,8,19008]{2,1,0:T(8,128)(2,1)S(1)} %copy-done, f32[8,8]{1,0:T(8,128)S(1)} %broadcast_add_fusion, f32[8,8]{1,0:T(8,128)S(1)} %psum.22, f32[8,8]{1,0:T(8,128)S(1)} %multiply_select_fusion, f32[8,8]{1,0:T(8,128)S(1)} %pmax.7), kind=kLoop, calls=%fused_computation.7 | loop fusion | flops 13229568 | bytes 5171200 | tf_op jit(solution)/shard_map/reduce_sum | solution.py:41
  80.4 4.2 %all-to-all-start.1 = ((f32[4,4,8]{2,1,0:T(4,128)}), f32[4,4,8]{2,1,0:T(4,128)S(1)}, u32[]{:S(2)}, u32[]{:S(2)}) async-start(f32[4,4,8]{2,1,0:T(4,128)} %bitcast.1), calls=%async_computation.1 | async-start | bytes 16384 | tf_op jit(solution)/shard_map/all_to_all | solution.py:70
  84.6 0.4 convolution_convert_fusion
  85.0 1.0 all_to_all.24
  86.0 3.3 %all-to-all-done.1 = f32[4,4,8]{2,1,0:T(4,128)S(1)} async-done(((f32[4,4,8]{2,1,0:T(4,128)}), f32[4,4,8]{2,1,0:T(4,128)S(1)}, u32[]{:S(2)}, u32[]{:S(2)}) %all-to-all-start.1) | async-done | bytes 544 | tf_op jit(solution)/shard_map/all_to_all | solution.py:70
  89.3 3.5 %all-to-all-start = ((bf16[4,4,19008]{2,1,0:T(4,128)(2,1)}), bf16[4,4,19008]{2,1,0:T(4,128)(2,1)S(1)}, u32[]{:S(2)}, u32[]{:S(2)}) async-start(bf16[4,4,19008]{2,1,0:T(4,128)(2,1)} %all_to_all.24), calls=%async_computation | async-start | bytes 1220608 | tf_op jit(solution)/shard_map/all_to_all | solution.py:66
  92.8 0.5 broadcast.35
  93.3 0.7 reduce.4
  93.9 0.6 all_to_all.32
  94.5 0.7 copy.13
  95.2 5.8 %all-to-all-done = bf16[4,4,19008]{2,1,0:T(4,128)(2,1)S(1)} async-done(((bf16[4,4,19008]{2,1,0:T(4,128)(2,1)}), bf16[4,4,19008]{2,1,0:T(4,128)(2,1)S(1)}, u32[]{:S(2)}, u32[]{:S(2)}) %all-to-all-start) | async-done | bytes 608288 | tf_op jit(solution)/shard_map/all_to_all | solution.py:66
  101.0 1.1 %all_to_all.26 = bf16[16,19008]{1,0:T(8,128)(2,1)} reshape(bf16[4,4,19008]{2,1,0:T(4,128)(2,1)S(1)} %all-to-all-done) | data formatting | bytes 1216512 | tf_op jit(solution)/shard_map/all_to_all | solution.py:66
  (17 shorter events, 0.7 us)
Async XLA Ops:
  0.6 22.0 %copy-start = (bf16[8,8,19008]{2,1,0:T(8,128)(2,1)S(1)}, bf16[8,8,19008]{2,1,0:T(8,128)(2,1)}, u32[]{:S(2)}) copy-start(bf16[8,8,19008]{2,1,0:T(8,128)(2,1)} %param.5) | copy-start | bytes 7299076
  0.6 22.0 %copy-start.1 = (s32[8,8]{1,0:T(8,128)S(1)}, s32[8,8]{1,0:T(8,128)}, u32[]{:S(2)}) copy-start(s32[8,8]{1,0:T(8,128)} %param.7) | copy-start | bytes 772
  37.9 17.8 %copy-start.2 = (s32[8]{0:T(128)S(1)}, s32[8]{0:T(128)}, u32[]{:S(2)}) copy-start(s32[8]{0:T(128)} %param.8) | copy-start | bytes 100
  56.8 23.5 %all-to-all-start.2 = ((f32[4,4,1]{1,2,0:T(1,128)}), f32[4,4,1]{1,2,0:T(1,128)S(1)}, u32[]{:S(2)}, u32[]{:S(2)}) async-start(f32[4,4,1]{1,2,0:T(1,128)} %bitcast.3), calls=%async_computation.2 | async-start | bytes 4096 | tf_op jit(solution)/shard_map/all_to_all | solution.py:71
  80.4 8.9 %all-to-all-start.1 = ((f32[4,4,8]{2,1,0:T(4,128)}), f32[4,4,8]{2,1,0:T(4,128)S(1)}, u32[]{:S(2)}, u32[]{:S(2)}) async-start(f32[4,4,8]{2,1,0:T(4,128)} %bitcast.1), calls=%async_computation.1 | async-start | bytes 16384 | tf_op jit(solution)/shard_map/all_to_all | solution.py:70
  89.3 11.8 %all-to-all-start = ((bf16[4,4,19008]{2,1,0:T(4,128)(2,1)}), bf16[4,4,19008]{2,1,0:T(4,128)(2,1)S(1)}, u32[]{:S(2)}, u32[]{:S(2)}) async-start(bf16[4,4,19008]{2,1,0:T(4,128)(2,1)} %all_to_all.24), calls=%async_computation | async-start | bytes 1220608 | tf_op jit(solution)/shard_map/all_to_all | solution.py:66
